TPU v7x, 64 devices: a 2x2x8 block of a 4x4x8 slice. The times are simulated.
64 devices in a mesh: dp: 4 (over x, y), ep: 16 (over z, core).
Axes of the slice: x: 2, y: 2, z: 8, core: 2. Of those that a mesh axis runs over, the one named last changes fastest.
The devices are a block of a 4x4x8 slice.
Arguments:
- hidden: bfloat16 [512, 1280], P(('dp', 'ep')), parts along dimension 0
- topk_idx: int32 [512, 6], P(('dp', 'ep')), parts along dimension 0
- w_router: bfloat16 [1280, 64], replicated
- w_gate: bfloat16 [64, 1280, 896], P('ep')
- w_up: bfloat16 [64, 1280, 896], P('ep')
- w_down: bfloat16 [64, 896, 1280], P('ep')
- shared_gate: bfloat16 [1280, 1792], replicated
- shared_up: bfloat16 [1280, 1792], replicated
- shared_down: bfloat16 [1792, 1280], replicated
Outputs:
- output: bfloat16 [512, 1280], P(('dp', 'ep')), parts along dimension 0
There are 4 independent parts. A program takes and returns all parts, laid end to end along the dimension named above; an argument that names none is the same for every part.
All inputs are finite; a program needn't handle non-finite values.
Results may differ from a plain program's by a relative error of at most 0.00646848.
Values are sent between devices in bfloat16 or wider.
A program may use at most 768 MiB of HBM per device.

v0:
```python
import jax
import jax.numpy as jnp
from jax import lax
from jax.sharding import PartitionSpec as P

GATE_SCALE = 16.0


def swiglu(rows, gate_mat, up_mat, down_mat):
    gate_val = jnp.dot(rows, gate_mat, preferred_element_type=jnp.float32)
    up_val = jnp.dot(rows, up_mat, preferred_element_type=jnp.float32)
    inner_act = (jax.nn.silu(gate_val) * up_val).astype(jnp.bfloat16)
    return jnp.dot(inner_act, down_mat, preferred_element_type=jnp.float32)


def sort_by_expert(row_ids, local_experts):
    num_rows = row_ids.shape[0]
    sort_key = jnp.where(row_ids < 0, local_experts, row_ids)
    sort_order = jnp.argsort(sort_key)
    expert_range = jnp.arange(local_experts, dtype=jnp.int32)
    group_sizes = jnp.sum((sort_key[:, None] == expert_range[None, :]).astype(jnp.int32), axis=0).astype(jnp.int32)
    inverse = jnp.zeros((num_rows,), jnp.int32).at[sort_order].set(jnp.arange(num_rows, dtype=jnp.int32))
    return sort_order, inverse, group_sizes


def expert_block(sorted_rows, group_sizes, w_gate, w_up, w_down):
    gate_val = lax.ragged_dot(sorted_rows, w_gate, group_sizes, preferred_element_type=jnp.float32)
    up_val = lax.ragged_dot(sorted_rows, w_up, group_sizes, preferred_element_type=jnp.float32)
    inner_act = (jax.nn.silu(gate_val) * up_val).astype(jnp.bfloat16)
    return lax.ragged_dot(inner_act, w_down, group_sizes, preferred_element_type=jnp.float32).astype(jnp.bfloat16)


def solution(mesh):
    group_size = mesh.shape['ep']
    row_spec = P(('dp', 'ep'), None)
    expert_spec = P('ep', None, None)

    def local_moe(hidden, topk_idx, w_router, w_gate, w_up, w_down, shared_gate, shared_up, shared_down):
        tok_rows, hidden_dim = hidden.shape
        top_k = topk_idx.shape[1]
        local_experts = w_gate.shape[0]
        logits = jnp.dot(hidden, w_router, preferred_element_type=jnp.float32)
        route_prob = jax.nn.softmax(logits, axis=-1)
        gate_weight = GATE_SCALE * jnp.take_along_axis(route_prob, topk_idx, axis=1)
        dest_dev = topk_idx // local_experts
        dev_ids = jnp.arange(group_size, dtype=jnp.int32)
        to_dest = dest_dev[None, :, :] == dev_ids[:, None, None]
        send_rows = jnp.where(to_dest[:, :, :, None], hidden[None, :, None, :], jnp.zeros((), jnp.bfloat16))
        send_rows = send_rows.reshape(group_size * tok_rows * top_k, hidden_dim)
        send_ids = jnp.where(to_dest, (topk_idx % local_experts)[None, :, :], -1).reshape(group_size * tok_rows * top_k)
        recv_rows = lax.all_to_all(send_rows, 'ep', 0, 0, tiled=True)
        recv_ids = lax.all_to_all(send_ids, 'ep', 0, 0, tiled=True)
        sort_order, inverse, group_sizes = sort_by_expert(recv_ids, local_experts)
        sorted_out = expert_block(jnp.take(recv_rows, sort_order, axis=0), group_sizes, w_gate, w_up, w_down)
        expert_rows = jnp.take(sorted_out, inverse, axis=0)
        back_rows = lax.all_to_all(expert_rows, 'ep', 0, 0, tiled=True)
        back_rows = back_rows.reshape(group_size, tok_rows, top_k, hidden_dim)
        chosen = jnp.sum(jnp.where(to_dest[:, :, :, None], back_rows, jnp.zeros((), jnp.bfloat16)), axis=0)
        routed = jnp.einsum('tk,tkd->td', gate_weight, chosen, preferred_element_type=jnp.float32)
        shared_out = swiglu(hidden, shared_gate, shared_up, shared_down)
        return (shared_out + routed).astype(jnp.bfloat16)

    return jax.shard_map(local_moe, mesh=mesh,
                         in_specs=(row_spec, row_spec, P(), expert_spec, expert_spec, expert_spec, P(), P(), P()),
                         out_specs=row_spec, check_vma=False)
```

profile of v0, /device:TPU:21, one launch (start us, length us, event | category | flops | bytes accessed | tf_op | source)
XLA Modules:
  0.0 175.0 jit_solution(8596153642537683554)
XLA Ops:
  0.0 0.0 copy-start
  0.0 0.7 add_select_fusion.1
  0.7 0.1 eq.50
  0.8 0.1 broadcast_in_dim.82
  0.9 0.6 compare_select_fusion
  1.5 10.7 %all-to-all-start.1 = ((s32[16,48,1]{1,2,0:T(1,128)}), s32[16,48,1]{1,2,0:T(1,128)S(1)}, u32[]{:S(2)}, u32[]{:S(2)}) async-start(s32[16,48,1]{1,2,0:T(1,128)} %compare_select_fusion), calls=%async_computation.1 | async-start | bytes 16384 | tf_op jit(solution)/shard_map/all_to_all | solution.py:52
  12.3 0.7 broadcast_in_dim.78
  13.1 1.5 broadcast_select_fusion.2
  14.5 4.6 %all-to-all-done.1 = s32[16,48,1]{1,2,0:T(1,128)S(1)} async-done(((s32[16,48,1]{1,2,0:T(1,128)}), s32[16,48,1]{1,2,0:T(1,128)S(1)}, u32[]{:S(2)}, u32[]{:S(2)}) %all-to-all-start.1) | async-done | bytes 3104 | tf_op jit(solution)/shard_map/all_to_all | solution.py:52
  19.1 4.2 %all-to-all-start = ((bf16[16,48,1280]{2,1,0:T(8,128)(2,1)}), bf16[16,48,1280]{2,1,0:T(8,128)(2,1)S(1)}, u32[]{:S(2)}, u32[]{:S(2)}) async-start(bf16[16,48,1280]{2,1,0:T(8,128)(2,1)} %broadcast_select_fusion.2), calls=%async_computation | async-start | bytes 3932160 | tf_op jit(solution)/shard_map/all_to_all | solution.py:51
  23.3 0.5 broadcast.136
  23.8 0.7 reduce.5
  24.5 0.1 all_to_all.21
  24.6 4.4 %sort.17 = (s32[768]{0:T(1024)}, s32[768]{0:T(1024)S(1)}) sort(s32[768]{0:T(1024)S(1)} %compare_select_fusion.3, s32[768]{0:T(1024)S(1)} %iota.19), dimensions={0}, to_apply=%region_2.0 | sort | flops 7680 | bytes 12288 | tf_op jit(solution)/shard_map/jit(argsort)/sort | solution.py:19
  28.9 0.6 convert_reduce_fusion
  29.6 1.4 ragged-dot-metadata
  30.9 3.4 %scatter_custom_fusion = s32[768]{0:T(1024)S(1)} fusion(s32[768]{0:T(1024)S(1)} %compare_select_fusion.2, s32[768]{0:T(1024)S(1)} %iota.20, s32[]{:T(128)} %constant.59.clone.1), kind=kCustom, calls=%fused_computation.44 | custom fusion | bytes 3076 | tf_op jit(solution)/shard_map/scatter | solution.py:22
  34.4 35.8 %all-to-all-done = bf16[16,48,1280]{2,1,0:T(8,128)(2,1)S(1)} async-done(((bf16[16,48,1280]{2,1,0:T(8,128)(2,1)}), bf16[16,48,1280]{2,1,0:T(8,128)(2,1)S(1)}, u32[]{:S(2)}, u32[]{:S(2)}) %all-to-all-start) | async-done | bytes 1966112 | tf_op jit(solution)/shard_map/all_to_all | solution.py:51
  70.2 3.7 %gather_fusion.1 = bf16[768,1280]{1,0:T(8,128)(2,1)} fusion(bf16[768,1280]{1,0:T(8,128)(2,1)S(1)} %bitcast.21, s32[1024]{0:T(1024)S(1)} %pad_clamp_fusion.1), kind=kCustom, calls=%fused_computation.clone | custom fusion | bytes 3935232 | tf_op jit(solution)/shard_map/jit(_take)/gather | solution.py:54
  73.9 3.1 %broadcast_select_fusion.1 = bf16[768,1280]{1,0:T(8,128)(2,1)} fusion(bf16[768,1280]{1,0:T(8,128)(2,1)} %gather_fusion.1, pred[768]{0:T(1024)(128)(4,1)S(1)} %compare_and_fusion.1), kind=kLoop, calls=%fused_computation.11 | loop fusion | flops 983040 | bytes 3932928 | tf_op jit(solution)/shard_map/jit(_take)/select_n | solution.py:54
  77.0 9.2 %ragged-dot-none.2 = f32[768,896]{1,0:T(8,128)} custom-call(s32[1]{0:T(128)} %get-tuple-element.8, s32[5]{0:T(128)} %get-tuple-element.9, s32[6]{0:T(128)} %get-tuple-element.10, s32[6]{0:T(128)} %get-tuple-element.11, s32[1]{0:T(128)} %get-tuple-element.8, bf16[768,1280]{1,0:T(8,128)(2,1)} %broadcast_select_fusion.1, bf16[4,1280,896]{2,1,0:T(8,128)(2,1)} %param.14), custom_call_target="tpu_custom_call" | custom-call | flops 1761607680 | bytes 13893648 | tf_op jit(solution)/shard_map/ragged_dot_general/ragged-dot-none
  86.2 0.0 copy-start.1
  86.2 9.4 %ragged-dot-none.1 = f32[768,896]{1,0:T(8,128)} custom-call(s32[1]{0:T(128)} %get-tuple-element.8, s32[5]{0:T(128)} %get-tuple-element.9, s32[6]{0:T(128)} %get-tuple-element.10, s32[6]{0:T(128)} %get-tuple-element.11, s32[1]{0:T(128)} %get-tuple-element.8, bf16[768,1280]{1,0:T(8,128)(2,1)} %broadcast_select_fusion.1, bf16[4,1280,896]{2,1,0:T(8,128)(2,1)} %param.15), custom_call_target="tpu_custom_call" | custom-call | flops 1761607680 | bytes 13893648 | tf_op jit(solution)/shard_map/ragged_dot_general/ragged-dot-none
  95.5 0.0 copy-done.1
  95.5 3.6 %multiply_convert_fusion = bf16[768,896]{1,0:T(8,128)(2,1)} fusion(f32[768,896]{1,0:T(8,128)} %ragged-dot-none.1, f32[768,896]{1,0:T(8,128)S(1)} %copy-done.1), kind=kLoop, calls=%fused_computation.4 | loop fusion | flops 4128768 | bytes 6881280 | tf_op jit(solution)/shard_map/convert_element_type | solution.py:29
  99.2 9.2 %ragged-dot-none = f32[768,1280]{1,0:T(8,128)} custom-call(s32[1]{0:T(128)} %get-tuple-element.8, s32[5]{0:T(128)} %get-tuple-element.9, s32[6]{0:T(128)} %get-tuple-element.10, s32[6]{0:T(128)} %get-tuple-element.11, s32[1]{0:T(128)} %get-tuple-element.8, bf16[768,896]{1,0:T(8,128)(2,1)} %multiply_convert_fusion, bf16[4,896,1280]{2,1,0:T(8,128)(2,1)} %param.16), custom_call_target="tpu_custom_call" | custom-call | flops 1761607680 | bytes 14483472 | tf_op jit(solution)/shard_map/ragged_dot_general/ragged-dot-none
  108.4 2.3 %convert_element_type.20 = bf16[768,1280]{1,0:T(8,128)(2,1)S(1)} convert(f32[768,1280]{1,0:T(8,128)} %ragged-dot-none) | non-fusion elementwise | flops 983040 | bytes 5898240 | tf_op jit(solution)/shard_map/convert_element_type | solution.py:30
  110.7 3.7 %gather_fusion.2 = bf16[768,1280]{1,0:T(8,128)(2,1)} fusion(bf16[768,1280]{1,0:T(8,128)(2,1)S(1)} %convert_element_type.20, s32[1024]{0:T(1024)S(1)} %pad_clamp_fusion), kind=kCustom, calls=%fused_computation.1.clone | custom fusion | bytes 3935232 | tf_op jit(solution)/shard_map/jit(_take)/gather | solution.py:55
  114.4 3.1 %broadcast_select_fusion = bf16[768,1280]{1,0:T(8,128)(2,1)} fusion(bf16[768,1280]{1,0:T(8,128)(2,1)} %gather_fusion.2, pred[768]{0:T(1024)(128)(4,1)S(1)} %compare_and_fusion), kind=kLoop, calls=%fused_computation.10 | loop fusion | flops 983040 | bytes 3932928 | tf_op jit(solution)/shard_map/jit(_take)/select_n | solution.py:55
  117.5 0.0 copy-start.3
  117.5 0.0 copy-start.2
  117.5 5.1 %all-to-all-start.2 = ((bf16[16,48,1280]{2,1,0:T(8,128)(2,1)}), bf16[16,48,1280]{2,1,0:T(8,128)(2,1)S(1)}, u32[]{:S(2)}, u32[]{:S(2)}) async-start(bf16[16,48,1280]{2,1,0:T(8,128)(2,1)} %bitcast.22), calls=%async_computation.2 | async-start | bytes 3932160 | tf_op jit(solution)/shard_map/all_to_all | solution.py:56
  122.6 0.0 copy-done.3
  122.6 0.1 reshape.134
  122.7 0.0 copy-done
  122.7 0.0 copy-done.2
  122.7 0.3 fusion.15
  122.9 0.2 fusion.10
  123.1 0.1 fusion.9
  123.2 0.9 gather_fusion
  124.1 0.1 reshape.137
  124.2 3.0 %fusion.16 = f32[8,1792]{1,0:T(8,128)S(1)} fusion(bf16[8,1280]{1,0:T(8,128)(2,1)S(1)} %copy-done.2, bf16[1280,1792]{1,0:T(8,128)(2,1)} %param.17), kind=kOutput, calls=%fused_computation.48 | convolution fusion | flops 36700160 | bytes 4665344 | tf_op jit(solution)/shard_map/dot_general | solution.py:10
  127.2 41.5 %all-to-all-done.2 = bf16[16,48,1280]{2,1,0:T(8,128)(2,1)S(1)} async-done(((bf16[16,48,1280]{2,1,0:T(8,128)(2,1)}), bf16[16,48,1280]{2,1,0:T(8,128)(2,1)S(1)}, u32[]{:S(2)}, u32[]{:S(2)}) %all-to-all-start.2) | async-done | bytes 1966112 | tf_op jit(solution)/shard_map/all_to_all | solution.py:56
  168.7 0.4 select_reduce_fusion
  169.1 0.2 fusion.17
  169.3 5.7 %fusion.1 = bf16[8,1280]{1,0:T(8,128)(2,1)} fusion(bf16[1792,1280]{1,0:T(8,128)(2,1)} %param.19, bf16[8,1280]{1,0:T(8,128)(2,1)S(1)} %copy-done.2, bf16[1280,1792]{1,0:T(8,128)(2,1)} %param.18, f32[8,1792]{1,0:T(8,128)S(1)} %fusion.16, f32[8,1,1280]{2,1,0:T(1,128)S(1)} %fusion.17), kind=kOutput, calls=%fused_computation.8 | convolution fusion | flops 73506816 | bytes 9314304 | tf_op jit(solution)/shard_map/dot_general | solution.py:13
  (14 shorter events, 0.2 us)
Async XLA Ops:
  0.0 122.7 %copy-start = (bf16[1280,64]{0,1:T(8,128)(2,1)S(1)}, bf16[1280,64]{0,1:T(8,128)(2,1)}, u32[]{:S(2)}) copy-start(bf16[1280,64]{0,1:T(8,128)(2,1)} %param.13) | copy-start | bytes 491524
  1.5 17.6 %all-to-all-start.1 = ((s32[16,48,1]{1,2,0:T(1,128)}), s32[16,48,1]{1,2,0:T(1,128)S(1)}, u32[]{:S(2)}, u32[]{:S(2)}) async-start(s32[16,48,1]{1,2,0:T(1,128)} %compare_select_fusion), calls=%async_computation.1 | async-start | bytes 16384 | tf_op jit(solution)/shard_map/all_to_all | solution.py:52
  19.1 51.0 %all-to-all-start = ((bf16[16,48,1280]{2,1,0:T(8,128)(2,1)}), bf16[16,48,1280]{2,1,0:T(8,128)(2,1)S(1)}, u32[]{:S(2)}, u32[]{:S(2)}) async-start(bf16[16,48,1280]{2,1,0:T(8,128)(2,1)} %broadcast_select_fusion.2), calls=%async_computation | async-start | bytes 3932160 | tf_op jit(solution)/shard_map/all_to_all | solution.py:51
  86.2 9.4 %copy-start.1 = (f32[768,896]{1,0:T(8,128)S(1)}, f32[768,896]{1,0:T(8,128)}, u32[]{:S(2)}) copy-start(f32[768,896]{1,0:T(8,128)} %ragged-dot-none.2) | copy-start | bytes 8257540
  117.5 5.1 %copy-start.3 = (s32[8,6]{1,0:T(8,128)S(1)}, s32[8,6]{1,0:T(8,128)}, u32[]{:S(2)}) copy-start(s32[8,6]{1,0:T(8,128)} %param.12) | copy-start | bytes 580
  117.5 5.2 %copy-start.2 = (bf16[8,1280]{1,0:T(8,128)(2,1)S(1)}, bf16[8,1280]{1,0:T(8,128)(2,1)}, u32[]{:S(2)}) copy-start(bf16[8,1280]{1,0:T(8,128)(2,1)} %param.11) | copy-start | bytes 61444
  117.5 51.2 %all-to-all-start.2 = ((bf16[16,48,1280]{2,1,0:T(8,128)(2,1)}), bf16[16,48,1280]{2,1,0:T(8,128)(2,1)S(1)}, u32[]{:S(2)}, u32[]{:S(2)}) async-start(bf16[16,48,1280]{2,1,0:T(8,128)(2,1)} %bitcast.22), calls=%async_computation.2 | async-start | bytes 3932160 | tf_op jit(solution)/shard_map/all_to_all | solution.py:56
where the time goes:
time: 176 us; the launch traced here: 175 us
  waiting for transfers between devices  81.8 us (46%)
  Pallas kernels  29.1 us (17%)
  other arithmetic  21.3 us (12%)
  starting transfers between devices  20 us (11%)
  local copies, waits for them, and re-layouts  13.5 us (8%)
  matrix products  9.18 us (5%)
    all_to_all x1, waiting for transfers between devices, local_moe(): back_rows = lax.all_to_all(expert_rows, 'ep', 0, 0, tiled=True)  41.5 us
    all_to_all x1, waiting for transfers between devices, local_moe(): recv_rows = lax.all_to_all(send_rows, 'ep', 0, 0, tiled=True)  35.8 us
    another operation x3, Pallas kernels  27.7 us
    all_to_all x1, starting transfers between devices, local_moe(): recv_ids = lax.all_to_all(send_ids, 'ep', 0, 0, tiled=True)  10.7 us
    dot_general x1, matrix products, swiglu(): return jnp.dot(inner_act, down_mat, preferred_element_type=jnp.float32)  5.72 us
    all_to_all x1, starting transfers between devices, local_moe(): back_rows = lax.all_to_all(expert_rows, 'ep', 0, 0, tiled=True)  5.08 us
    all_to_all x1, waiting for transfers between devices, local_moe(): recv_ids = lax.all_to_all(send_ids, 'ep', 0, 0, tiled=True)  4.58 us
    sort x1, other arithmetic, sort_by_expert(): sort_order = jnp.argsort(sort_key)  4.37 us
  transfers between devices with their start and end apart: 3, of which 3 were waited for; matrix products, arithmetic and copies ran while one was open for 9% of the time, Pallas kernels for 1%

commit v1 on v0

v1 whole, which is shorter than its diff:
```python
import functools

import jax
import jax.numpy as jnp
from jax import lax
from jax.experimental import pallas as pl
from jax.experimental.pallas import tpu as pltpu
from jax.sharding import PartitionSpec as P

GATE_SCALE = 16.0
MESH = pl.DeviceIdType.MESH
LANES = 128
BLOCK = 256


def silu_mul(gate_val, up_val):
    return (gate_val / (1.0 + jnp.exp(-gate_val)) * up_val).astype(jnp.bfloat16)


def dot(lhs, rhs):
    return jnp.dot(lhs, rhs, preferred_element_type=jnp.float32)


def moe_kernel(n, hidden, idx, wr, wg, wu, wd, sg, su, sd, out,
               x_buf, id_buf, wr_buf, wg_buf, wu_buf, wd_buf, sg_buf, su_buf, sd_buf,
               h_buf, hs_buf, gate_buf, part, recv,
               in_sems, w_sems, s_sems, xs_sem, xr_sem, is_sem, ir_sem, ps_sem, pr_sem):
    me = lax.axis_index('ep')
    tok_rows = hidden.shape[0]
    local_experts, hidden_dim, ff = wg.shape
    shared_blocks = sg.shape[1] // LANES
    full = ff // BLOCK * BLOCK

    barrier = pltpu.get_barrier_semaphore()
    for d in range(1, n):
        pl.semaphore_signal(barrier, inc=1, device_id={'ep': lax.rem(me + d, n)}, device_id_type=MESH)

    my_rows = pl.ds(pl.multiple_of(me * tok_rows, tok_rows), tok_rows)
    copy_x = pltpu.make_async_copy(hidden, x_buf.at[my_rows], in_sems.at[0])
    copy_i = pltpu.make_async_copy(idx, id_buf.at[my_rows], in_sems.at[1])
    copy_r = pltpu.make_async_copy(wr, wr_buf, in_sems.at[2])
    copy_x.start()
    copy_i.start()
    copy_r.start()
    shared_id = jnp.minimum(me, shared_blocks - 1)
    cols = pl.ds(pl.multiple_of(shared_id * LANES, LANES), LANES)
    copy_s = [pltpu.make_async_copy(sg.at[:, cols], sg_buf, s_sems.at[0]),
              pltpu.make_async_copy(su.at[:, cols], su_buf, s_sems.at[1]),
              pltpu.make_async_copy(sd.at[cols], sd_buf, s_sems.at[2])]
    for c in copy_s:
        c.start()
    copy_g = [pltpu.make_async_copy(wg.at[e], wg_buf.at[e], w_sems.at[0, e]) for e in range(local_experts)]
    copy_u = [pltpu.make_async_copy(wu.at[e], wu_buf.at[e], w_sems.at[1, e]) for e in range(local_experts)]
    copy_d = [pltpu.make_async_copy(wd.at[e], wd_buf.at[e], w_sems.at[2, e]) for e in range(local_experts)]
    for e in range(local_experts):
        copy_g[e].start()
        copy_u[e].start()
    for e in range(local_experts):
        copy_d[e].start()

    copy_x.wait()
    copy_i.wait()
    pl.semaphore_wait(barrier, n - 1)
    x_sends, i_sends = [], []
    for d in range(1, n):
        peer = {'ep': lax.rem(me + d, n)}
        x_sends.append(pltpu.make_async_remote_copy(
            x_buf.at[my_rows], x_buf.at[my_rows], xs_sem.at[d], xr_sem.at[d], device_id=peer, device_id_type=MESH))
        i_sends.append(pltpu.make_async_remote_copy(
            id_buf.at[my_rows], id_buf.at[my_rows], is_sem.at[d], ir_sem.at[d], device_id=peer, device_id_type=MESH))
    for c in x_sends:
        c.start()
    for c in i_sends:
        c.start()
    for c in x_sends:
        c.wait()
    for c in i_sends:
        c.wait()

    copy_r.wait()
    logits = dot(x_buf[...], wr_buf[...])
    expd = jnp.exp(logits - jnp.max(logits, axis=-1, keepdims=True))
    prob = expd / jnp.sum(expd, axis=-1, keepdims=True)
    lane_expert = lax.broadcasted_iota(jnp.int32, prob.shape, 1)
    ids = id_buf[...]
    for e in range(local_experts):
        expert = me * local_experts + e
        gate = GATE_SCALE * jnp.sum(jnp.where(lane_expert == expert, prob, 0.0), axis=-1, keepdims=True)
        hit = jnp.sum((ids == expert).astype(jnp.float32), axis=-1, keepdims=True)
        gate_buf[e] = jnp.broadcast_to(jnp.where(hit > 0.0, gate, -1.0), gate_buf.shape[1:])

    copy_s[0].wait()
    copy_s[1].wait()
    both = dot(x_buf[...], jnp.concatenate([sg_buf[...], su_buf[...]], axis=1))
    inner = silu_mul(both[:, :LANES], both[:, LANES:])
    hs_buf[...] = jnp.where(me < shared_blocks, inner, jnp.zeros_like(inner))

    for e in range(local_experts):
        copy_g[e].wait()
        copy_u[e].wait()
        for lo in range(0, full, BLOCK):
            gate_val = dot(x_buf[...], wg_buf[e, :, lo:lo + BLOCK])
            up_val = dot(x_buf[...], wu_buf[e, :, lo:lo + BLOCK])
            h_buf[e, :, lo:lo + BLOCK] = silu_mul(gate_val, up_val)
        if full < ff:
            both = dot(x_buf[...], jnp.concatenate([wg_buf[e, :, full:], wu_buf[e, :, full:]], axis=1))
            h_buf[e, :, full:] = silu_mul(both[:, :ff - full], both[:, ff - full:])

    copy_s[2].wait()
    for e in range(local_experts):
        copy_d[e].wait()
    for lo in range(0, hidden_dim, BLOCK):
        acc = dot(hs_buf[...], sd_buf[:, lo:lo + BLOCK])
        for e in range(local_experts):
            val = dot(h_buf[e], wd_buf[e, :, lo:lo + BLOCK]).astype(jnp.bfloat16).astype(jnp.float32)
            gate = jnp.concatenate([gate_buf[e]] * (BLOCK // LANES), axis=1)
            acc += jnp.where(gate >= 0.0, gate * val, 0.0)
        part[:, lo:lo + BLOCK] = acc

    p_sends = []
    for d in range(1, n):
        peer = lax.rem(me + d, n)
        rows = pl.ds(pl.multiple_of(peer * tok_rows, tok_rows), tok_rows)
        p_sends.append(pltpu.make_async_remote_copy(
            part.at[rows], recv.at[d], ps_sem.at[d], pr_sem.at[d], device_id={'ep': peer}, device_id_type=MESH))
        p_sends[-1].start()
    total = part[my_rows]
    for d, c in enumerate(p_sends, 1):
        c.wait_recv()
        total += recv[d]
    out[...] = total.astype(out.dtype)
    for c in p_sends:
        c.wait_send()


def solution(mesh):
    group_size = mesh.shape['ep']
    row_spec = P(('dp', 'ep'), None)
    expert_spec = P('ep', None, None)

    def local_moe(hidden, topk_idx, w_router, w_gate, w_up, w_down, shared_gate, shared_up, shared_down):
        tok_rows, hidden_dim = hidden.shape
        top_k = topk_idx.shape[1]
        local_experts, _, ff = w_gate.shape
        rows = tok_rows * group_size
        bf16 = jnp.bfloat16
        any_spec = pl.BlockSpec(memory_space=pl.ANY)
        dma = pltpu.SemaphoreType.DMA
        return pl.pallas_call(
            functools.partial(moe_kernel, group_size),
            out_shape=jax.ShapeDtypeStruct((tok_rows, hidden_dim), bf16),
            in_specs=[any_spec] * 9,
            out_specs=pl.BlockSpec(memory_space=pltpu.VMEM),
            scratch_shapes=[
                pltpu.VMEM((rows, hidden_dim), bf16),
                pltpu.VMEM((rows, top_k), jnp.int32),
                pltpu.VMEM(w_router.shape, bf16),
                pltpu.VMEM(w_gate.shape, bf16),
                pltpu.VMEM(w_up.shape, bf16),
                pltpu.VMEM(w_down.shape, bf16),
                pltpu.VMEM((hidden_dim, LANES), bf16),
                pltpu.VMEM((hidden_dim, LANES), bf16),
                pltpu.VMEM((LANES, hidden_dim), bf16),
                pltpu.VMEM((local_experts, rows, ff), bf16),
                pltpu.VMEM((rows, LANES), bf16),
                pltpu.VMEM((local_experts, rows, LANES), jnp.float32),
                pltpu.VMEM((rows, hidden_dim), jnp.float32),
                pltpu.VMEM((group_size, tok_rows, hidden_dim), jnp.float32),
                dma((3,)), dma((3, local_experts)), dma((3,)),
                dma((group_size,)), dma((group_size,)), dma((group_size,)), dma((group_size,)),
                dma((group_size,)), dma((group_size,)),
            ],
            compiler_params=pltpu.CompilerParams(
                collective_id=0, has_side_effects=True, vmem_limit_bytes=56 * 1024 * 1024),
            name='moe_step',
        )(hidden, topk_idx, w_router, w_gate, w_up, w_down, shared_gate, shared_up, shared_down)

    return jax.shard_map(local_moe, mesh=mesh,
                         in_specs=(row_spec, row_spec, P(), expert_spec, expert_spec, expert_spec, P(), P(), P()),
                         out_specs=row_spec, check_vma=False)
```

time: 176 us -> 53.4 us (0.30)
  waiting for transfers between devices: 81.8 us -> 0 us
  other arithmetic: 21.3 us -> 0 us
  Pallas kernels: 29.1 us -> 50.1 us
  starting transfers between devices: 20 us -> 0 us
  local copies, waits for them, and re-layouts: 13.5 us -> 3.14 us
  matrix products: 9.18 us -> 0 us
    all_to_all x3 -> x0, waiting for transfers between devices: 81.8 us -> none  [the longest x1 41.5 us: local_moe(): back_rows = lax.all_to_all(expert_rows, 'ep', 0, 0, tiled=True)]
    pallas_call x0 -> x1, Pallas kernels: none -> 50.1 us  [local_moe(): pl.pallas_call(functools.partial(moe_kernel, group_size), out_shape=jax.S...]
    another operation x3 -> x0, Pallas kernels: 27.7 us -> none
    all_to_all x3 -> x0, starting transfers between devices: 20 us -> none  [the longest x1 10.7 us: local_moe(): recv_ids = lax.all_to_all(send_ids, 'ep', 0, 0, tiled=True)]
    dot_general x4 -> x0, matrix products: 9.18 us -> none  [the longest x1 5.72 us: swiglu(): return jnp.dot(inner_act, down_mat, preferred_element_type=jnp.float32)]
    select_n x8 -> x0, other arithmetic: 9.01 us -> none  [the longest x1 3.1 us: local_moe(): jnp.take(recv_rows, sort_order, axis=0)]
    gather x5 -> x0, local copies, waits for them, and re-layouts: 8.48 us -> none  [the longest x1 3.72 us: local_moe(): jnp.take(recv_rows, sort_order, axis=0)]
    convert_element_type x2 -> x0, other arithmetic: 5.93 us -> none  [the longest x1 3.63 us: expert_block(): inner_act = (jax.nn.silu(gate_val) * up_val).astype(jnp.bfloat16)]
  transfers between devices with their start and end apart: 3 -> 0, of which waited for: 3 -> 0; matrix products, arithmetic and copies ran while one was open for 9% -> 0% of each run, Pallas kernels for 1% -> 0%
where the time goes in v1:
time: 53.4 us; the launch traced here: 53.3 us
  Pallas kernels  50.1 us (94%)
  local copies, waits for them, and re-layouts  3.14 us (6%)
    pallas_call x1, Pallas kernels, local_moe(): pl.pallas_call(functools.partial(moe_kernel, group_size), out_shape=jax.S...  50.1 us
    unnamed x2, local copies, waits for them, and re-layouts  3.14 us

profile of v1, /device:TPU:21, one launch (start us, length us, event | category | flops | bytes accessed | tf_op | source)
XLA Modules:
  0.0 53.3 jit_solution(8391207289901470152)
XLA Ops:
  0.0 1.8 %copy.10.wr = bf16[1280,64]{1,0:T(8,128)(2,1)} copy(bf16[1280,64]{0,1:T(8,128)(2,1)} %param.11) | data formatting | bytes 327680 | tf_op args[2]
  1.8 50.1 %moe_step.1 = bf16[8,1280]{1,0:T(8,128)(2,1)} custom-call(bf16[8,1280]{1,0:T(8,128)(2,1)} %hidden.1, s32[8,6]{1,0:T(8,128)} %idx.1, bf16[1280,64]{1,0:T(8,128)(2,1)} %copy.10.wr, bf16[4,1280,896]{2,1,0:T(8,128)(2,1)} %wg.1, bf16[4,1280,896]{2,1,0:T(8,128)(2,1)} %wu.1, bf16[4,896,1280]{2,1,0:T(8,128)(2,1)} %wd.1, bf16[1280,1792]{1,0:T(8,128)(2,1)} %sg.1, ...), custom_call_target="tpu_custom_call" | custom-call | tf_op jit(solution)/shard_map/moe_step/pallas_call | solution.py:149
  51.9 1.3 %copy.12 = bf16[8,1280]{1,0:T(8,128)(2,1)} copy(bf16[8,1280]{1,0:T(8,128)(2,1)} %moe_step.1) | data formatting | bytes 40960
